TPU v7x, 128 devices: a whole 4x4x4 slice. The times are simulated.
128 devices in a mesh: patch: 16 (over y, z), hidden: 8 (over x, core).
Axes of the slice: x: 4, y: 4, z: 4, core: 2. Of those that a mesh axis runs over, the one named last changes fastest.
Arguments:
- grid_latent: bfloat16 [49152, 512], P('patch'), may hold values from -6 to 6
- mesh_latent: bfloat16 [81920, 512], P('patch'), may hold values from -6 to 6
- edge_latent: bfloat16 [131072, 512], P('patch'), may hold values from -6 to 6
- senders: int32 [131072], P('patch'), may hold values from 0 to 49151, as said below
- receivers: int32 [131072], P('patch'), may hold values from 0 to 81919
- mesh_slot: int32 [81920], replicated, may hold values from 0 to 81919, as said below
- edge_counts: int32 [16], P('patch'), may hold values from 2730 to 8192, as said below
- w_edge: bfloat16 [512, 512], P(None, 'hidden'), may hold values from -0.25 to 0.25
- w_sender: bfloat16 [512, 512], P(None, 'hidden'), may hold values from -0.25 to 0.25
- w_receiver: bfloat16 [512, 512], P(None, 'hidden'), may hold values from -0.25 to 0.25
- edge_bias: float32 [512], P('hidden'), may hold values from -3 to 3
- w_edge_out: bfloat16 [512, 512], P('hidden'), may hold values from -0.25 to 0.25
- edge_out_bias: float32 [512], P('hidden'), may hold values from -3 to 3
- edge_gain: float32 [512], P('hidden'), may hold values from 0.25 to 1.75
- edge_shift: float32 [512], P('hidden'), may hold values from -2 to 2
- w_mesh_in: bfloat16 [512, 512], P(None, 'hidden'), may hold values from -0.25 to 0.25
- w_message_in: bfloat16 [512, 512], P(None, 'hidden'), may hold values from -0.25 to 0.25
- mesh_bias: float32 [512], P('hidden'), may hold values from -3 to 3
- w_mesh_out: bfloat16 [512, 512], P('hidden'), may hold values from -0.25 to 0.25
- mesh_out_bias: float32 [512], P('hidden'), may hold values from -3 to 3
- mesh_gain: float32 [512], P('hidden'), may hold values from 0.25 to 1.75
- mesh_shift: float32 [512], P('hidden'), may hold values from -2 to 2
Outputs:
- mesh_out: bfloat16 [81920, 512], P('patch', 'hidden')
- edge_out: bfloat16 [131072, 512], P('patch', 'hidden')
Inputs may be any that keep to these rules, and one draw needn't show every extreme that they name: `mesh_slot`: A permutation of the mesh node ids 0 to 81919; owner block p holds mesh rows p * 5120 to (p + 1) * 5120 - 1. `senders`: edge slots of block p (slots p * 8192 to (p + 1) * 8192 - 1) send from grid nodes p * 3072 to (p + 1) * 3072 - 1. Only the first edge_counts[p] slots of block p are live; some block is full.
All inputs are finite; a program needn't handle non-finite values.
Results may differ from a plain program's by a relative error of at most 0.014.
Values may be sent and summed in bfloat16 or wider, within the bound.
No kernel may reach another device: no remote copies, remote signals or barrier semaphores. Data moves between devices by JAX's collectives and lax.ppermute only.
A program may use at most 192 MiB of HBM per device.

v0:
```python
import jax
import jax.numpy as jnp
from jax import lax
from jax.experimental import pallas as pl
from jax.experimental.pallas import tpu as pltpu
from jax.sharding import PartitionSpec as P


EPSILON = 1e-05
LANES = 128
BF = jnp.bfloat16
F32 = jnp.float32
I32 = jnp.int32

NP = 16
NH = 8
D = 512
E = 8192
G = 3072
M = 5120
ML = M // NH
ROWS = E // LANES
N1 = 1152
HALF = N1 // 2
CA = 64
CX = 160
CS = 384
FLAG = 16
MESH_AT = HALF + FLAG
OUT_ROWS = MESH_AT + ML // 2
OP = NP * CA
OM = OP + 256
OS = OM + 256
NS = OS + CS
WIN = 64
VROW = 128
WROWS = VROW + 8
STEP = 128
VMEM = 60 * 1024 * 1024


def dot(a, b):
    return jnp.dot(a, b, preferred_element_type=F32)


def dot_nt(a, b):
    return lax.dot_general(a, b, (((1,), (1,)), ((), ())), preferred_element_type=F32)


def iota(shape, axis):
    return lax.broadcasted_iota(I32, shape, axis)


def onehot(cond):
    return jnp.where(cond, 1.0, 0.0).astype(BF)


def lane_join(a, b):
    low = iota(a.shape, 1) < 64
    return jnp.where(low, a, pltpu.roll(b, 64, 1)), jnp.where(low, pltpu.roll(a, 64, 1), b)


def silu(v):
    return v / (1.0 + jnp.exp(-v))


def normalized(v, gain, shift):
    mean = jnp.mean(v, axis=1, keepdims=True)
    c = v - mean
    var = jnp.mean(c * c, axis=1, keepdims=True)
    return c * lax.rsqrt(var + EPSILON) * gain + shift


def row_of(x):
    return jnp.concatenate([x[i : i + 1, :] for i in range(x.shape[0])], axis=1)


def gather_kernel(
    count_ref, where_ref, recv_ref, slots_ref, send_ref, edge_hbm, grid_hbm,
    key_ref, starts_ref, list_ref, sent_ref, info_ref, slot_ref, slot_row_ref, tgt,
    table, hits, known, starts, edge, grid, acc, meta, edge_sem, grid_sem, starts_sem,
):
    chunk = lambda i: pltpu.make_async_copy(
        edge_hbm.at[pl.ds(i * 1024, 1024)], edge.at[pl.ds(i * 1024, 1024)], edge_sem.at[i]
    )
    for i in range(8):
        chunk(i).start()
    grid_copy = pltpu.make_async_copy(grid_hbm, grid, grid_sem)
    grid_copy.start()
    own = where_ref[0]
    patch = where_ref[1]
    v = slots_ref[...]
    table[:, 0:128] = ((v >> 8) - 160).astype(F32).astype(BF)
    table[:, 128:256] = (v & 255).astype(F32).astype(BF)

    def group(g, carry):
        r = recv_ref[pl.ds(pl.multiple_of(g * 8, 8), 8), :]
        hi = (r >> 7).astype(F32).T
        lo = (r & 127).astype(F32).T
        rows = iota((128, 640), 1).astype(F32)
        for j in range(8):
            hits[128 * j : 128 * j + 128, :] = onehot(rows == hi[:, j : j + 1])
        y = dot(hits[...], table[...])
        full = (y[:, 0:128] + 160.0) * 256.0 + y[:, 128:256]
        lane = iota((128, 128), 1).astype(F32)
        which = iota((128, 8), 1)
        got = jnp.zeros((128, 8), F32)
        for j in range(8):
            part = jnp.where(lane == lo[:, j : j + 1], full[128 * j : 128 * j + 128], 0.0)
            got = jnp.where(which == j, jnp.sum(part, axis=1, keepdims=True), got)
        tgt[pl.ds(pl.multiple_of(g * 8, 8), 8), :] = got.T
        return carry

    lax.fori_loop(0, ROWS // 8, group, 0)
    t = tgt[...]
    block = jnp.floor((t + 0.5) * (1.0 / ML))
    l = t - block * ML
    q = jnp.floor((block + 0.5) * (1.0 / NH))
    h = block - q * NH
    position = iota((ROWS, 128), 0) * 128 + iota((ROWS, 128), 1)
    live = position < count_ref[0]
    upper = onehot(iota((128, 128), 0) < iota((128, 128), 1))
    big = NH * ROWS
    row, col = iota((big, big), 0), iota((big, big), 1)
    lower = onehot((col < row) & ((col >> 6) == (row >> 6)))
    mine = [live & (h == float(k)) for k in range(NH)]
    mask = jnp.concatenate([onehot(m) for m in mine], axis=0)
    before_all = dot(mask, upper)
    counts_all = dot(mask, jnp.ones((128, 128), BF))
    above_all = dot(lower, counts_all.astype(BF))
    c = jnp.full((ROWS, 128), -1.0, F32)
    delta = jnp.full((ROWS, 128), -1.0, F32)
    begin = jnp.zeros((ROWS, 128), F32)
    totals = jnp.zeros((8, 128), F32)
    lane64 = iota((ROWS, 128), 1)
    lane8 = iota((8, 128), 1)
    for k in range(NH):
        at = slice(ROWS * k, ROWS * k + ROWS)
        above = above_all[at]
        place = before_all[at] + above
        start = jnp.floor(above * (1.0 / 16.0)) * 16.0
        c = jnp.where(mine[k], place, c)
        delta = jnp.where(mine[k], place - start, delta)
        begin = jnp.where(lane64 == k, start, begin)
        total = above[ROWS - 1 : ROWS, :] + counts_all[at][ROWS - 1 : ROWS, :]
        totals = jnp.where(lane8 == k, total, totals)
    key_ref[...] = jnp.where(delta >= 0.0, h * 256.0 + delta, -1.0)
    starts_ref[0:ROWS, :] = begin.astype(I32)
    spread = jnp.where(jnp.max(delta) >= WIN, 1.0, 0.0)
    starts_ref[ROWS : ROWS + 8, :] = totals.astype(I32)
    to_scalars = pltpu.make_async_copy(starts_ref, starts, starts_sem)
    to_scalars.start()
    acc[...] = jnp.zeros_like(acc)
    meta[...] = jnp.zeros_like(meta)
    s = (send_ref[...] - patch * G).astype(F32)
    s_hi = jnp.floor(s * (1.0 / 256.0))
    l_hi = jnp.floor(l * (1.0 / 256.0))
    kinds = [s_hi, s - 256.0 * s_hi, q, l_hi, l - 256.0 * l_hi, jnp.ones((ROWS, 128), F32)]
    kinds.append(jnp.where(h == own.astype(F32), c, -1.0))
    for k, x in enumerate(kinds):
        known[k] = x
    to_scalars.wait()
    total = starts[ROWS, own]

    def compact(i, carry):
        @pl.when(i % 2 == 0)
        def _():
            chunk(i // 2).wait()

        parts = [known[k, pl.ds(pl.multiple_of(8 * (i // 2), 8), 8), :] for k in range(7)]
        odd = i % 2 == 1
        parts = [jnp.where(odd, x[4:8], x[0:4]) for x in parts]
        c_row = row_of(parts[6])
        facts = jnp.concatenate([row_of(x) for x in parts[:6]] + [jnp.zeros((2, 512), F32)], axis=0).astype(BF)
        source = pl.ds(pl.multiple_of(512 * i, 512), 512)
        first = starts[4 * i, own]
        last = jnp.where(i == 15, total, starts[jnp.minimum(4 * i + 4, ROWS - 1), own] + 16)
        rounds = (jnp.minimum(last, N1) - first + STEP - 1) // STEP

        def add(k, carry):
            at = pl.multiple_of(first + STEP * k, 16)
            hit = onehot(c_row == (iota((STEP, 512), 0) + at).astype(F32))
            acc[pl.ds(at, STEP), :] += dot(hit, edge[source, :])
            meta[pl.ds(at, STEP), :] += dot_nt(hit, facts)
            return carry

        lax.fori_loop(0, rounds, add, 0)
        return carry

    lax.fori_loop(0, 16, compact, 0)
    grid_copy.wait()
    T = 384
    lower = onehot(iota((T, T), 1) < iota((T, T), 0))

    def place(i, state):
        carry, bad = state
        at = pl.ds(pl.multiple_of(T * i, T), T)
        facts = meta[at, :]
        valid = facts[:, 5:6] > 0.5
        sender = jnp.where(valid, facts[:, 0:1] * 256.0 + facts[:, 1:2], -1.0)
        hit = onehot(iota((T, G), 1).astype(F32) == sender)
        sent_ref[at, :] = dot(hit, grid[...]).astype(BF)
        list_ref[at, :] = acc[at, :].astype(BF)
        lane = iota((T, 128), 1)
        info = jnp.where(lane == 0, facts[:, 3:4], jnp.where(lane == 1, facts[:, 4:5], 0.0))
        info_ref[at, :] = jnp.where(lane == 2, 1.0, info).astype(BF)
        owner = jnp.where((lane.astype(F32) == facts[:, 2:3]) & valid, 1.0, 0.0)
        rank = jnp.sum(owner * (dot(lower, owner.astype(BF)) + carry), axis=1, keepdims=True)
        carry = carry + jnp.sum(owner, axis=0, keepdims=True)
        d = facts[:, 2:3] - patch.astype(F32)
        d = jnp.where(d < 0.0, d + NP, d)
        more = rank - CA
        slot = jnp.where((d == 1.0) & (more < CX), OP + more, -1.0)
        slot = jnp.where((d == NP - 1.0) & (more < CX), OM + more, slot)
        slot = jnp.where(rank < CA, facts[:, 2:3] * CA + rank, slot)
        slot = jnp.where(d == 0.0, jnp.where(rank < CS, OS + rank, -1.0), slot)
        bad = jnp.maximum(bad, jnp.max(jnp.where(valid & (slot < 0.0), 1.0, 0.0)))
        slots = jnp.broadcast_to(jnp.where(valid, slot, -1.0), (T, 128))
        slot_ref[at, :] = slots[:, 0:8]
        slot_row_ref[:, at] = slots.T[0:8, :]
        return carry, bad

    bad = jnp.maximum(jnp.where(total > N1, 1.0, 0.0), spread)
    _, bad = lax.fori_loop(0, N1 // T, place, (jnp.zeros((1, 128), F32), bad))
    slot_row_ref[:, N1 : N1 + 128] = jnp.broadcast_to(bad, (8, 128))


def gather(count, where, receivers, mesh_slot, senders, edge_latent, grid_latent):
    sds = jax.ShapeDtypeStruct
    smem = pl.BlockSpec(memory_space=pltpu.SMEM)
    vmem = pl.BlockSpec(memory_space=pltpu.VMEM)
    hbm = pl.BlockSpec(memory_space=pl.ANY)
    return pl.pallas_call(
        gather_kernel,
        out_shape=(
            sds((ROWS, 128), F32), sds((ROWS + 8, 128), I32),
            sds((N1, D), BF), sds((N1, D), BF), sds((N1, 128), BF), sds((N1, 8), F32), sds((8, N1 + 128), F32),
            sds((ROWS, 128), F32),
        ),
        in_specs=[smem, smem, vmem, vmem, vmem, hbm, hbm],
        scratch_shapes=[
            pltpu.VMEM((640, 256), BF),
            pltpu.VMEM((1024, 640), BF),
            pltpu.VMEM((7, ROWS, 128), F32),
            pltpu.SMEM((ROWS + 8, 128), I32),
            pltpu.VMEM((E, D), BF),
            pltpu.VMEM((G, D), BF),
            pltpu.VMEM((N1 + STEP, D), F32),
            pltpu.VMEM((N1 + STEP, 8), F32),
            pltpu.SemaphoreType.DMA((8,)),
            pltpu.SemaphoreType.DMA(()),
            pltpu.SemaphoreType.DMA(()),
        ],
        compiler_params=pltpu.CompilerParams(vmem_limit_bytes=VMEM),
        name="gather",
    )(
        count, where, receivers.reshape(ROWS, 128), mesh_slot.reshape(640, 128), senders.reshape(ROWS, 128),
        edge_latent, grid_latent,
    )


def walk_of(own):
    x, core = own // 2, own % 2
    places = [2 * ((x + 4 - k) % 4) for k in range(4)]
    return [p + core for p in places] + [p + 1 - core for p in places]


def vectors_of(v_ref, m, order=tuple(range(NH))):
    pairs = []
    for k in range(NH // 2):
        at = slice(128 * m, 128 * m + 128)
        x, y = v_ref[order[2 * k], :, at].astype(F32), v_ref[order[2 * k + 1], :, at].astype(F32)
        pairs.append(lane_join(x, y))
    rows = [jnp.concatenate([p[i] for p in pairs], axis=1) for i in range(2)]
    return [r[0:1] + r[1:2] + r[2:3] for r in rows]


def stack_kernel(e, s, r, mi, mm, eo, mo, *refs):
    vectors, (first_ref, second_ref) = refs[:8], refs[8:]
    for k, w in enumerate((r, mi, mm, eo, mo)):
        second_ref[64 * k : 64 * k + 64, :] = w[...]
    v = jnp.concatenate([x[...] for x in vectors], axis=1)
    v = jnp.broadcast_to(v, (8, D))
    hi = v.astype(BF)
    v = v - hi.astype(F32)
    mid = v.astype(BF)
    low = (v - mid.astype(F32)).astype(BF)
    row = iota((8, D), 0)
    parts = jnp.where(row == 0, hi.astype(F32), jnp.where(row == 1, mid.astype(F32), low.astype(F32)))
    parts = jnp.where(row < 3, parts, 0.0).astype(BF)
    for n in range(NH):
        first_ref[n, 0:64, :] = e[...]
        first_ref[n, 64:128, :] = s[...]
        first_ref[n, VROW:WROWS, :] = parts


def stacked(*args):
    return pl.pallas_call(
        stack_kernel,
        out_shape=(jax.ShapeDtypeStruct((NH, WROWS, D), BF), jax.ShapeDtypeStruct((320, D), BF)),
        name="stacked",
    )(*args)


def to_all(first, second):
    first = lax.all_to_all(first, "hidden", split_axis=0, concat_axis=0, tiled=True)
    walk = [second]
    for k in (1, 2, 3):
        walk.append(lax.ppermute(second, "hidden", [(i, (i + 2 * k) % NH) for i in range(NH)]))
    walk = jnp.stack(walk)
    other = lax.ppermute(walk, "hidden", [(i, i ^ 1) for i in range(NH)])
    return first, walk, other


def pack_kernel(where_ref, list_ref, sent_ref, info_ref, slot_row_ref, first_ref, oa_ref, op_ref, om_ref, pre, wide):
    order = walk_of(where_ref[0])
    w_edge = jnp.concatenate([first_ref[n, 0:64, :] for n in order], axis=0)
    w_sender = jnp.concatenate([first_ref[n, 64:128, :] for n in order], axis=0)
    bias = vectors_of(first_ref.at[:, VROW:WROWS], 0, order)[0]
    T = 384

    def first_layer(i, carry):
        at = pl.ds(pl.multiple_of(T * i, T), T)
        pre[at, 0:D] = (dot_nt(list_ref[at, :], w_edge) + dot_nt(sent_ref[at, :], w_sender) + bias).astype(BF)
        return carry

    lax.fori_loop(0, N1 // T, first_layer, 0)
    pre[:, D : D + 128] = info_ref[...]

    def spread(i, carry):
        hit = onehot((iota((T, N1), 0) + T * i).astype(F32) == slot_row_ref[0:1, 0:N1])
        wide[pl.ds(pl.multiple_of(T * i, T), T), :] = dot(hit, pre[...])
        return carry

    lax.fori_loop(0, OS // T, spread, 0)
    kind = iota((8, 128), 0)
    bad = slot_row_ref[0:8, N1 : N1 + 128]

    def facts_of(at):
        return jnp.where(kind == 3, bad, wide[at : at + 128, D : D + 128].T[0:8, :])

    for i in range(NP // 2):
        x = facts_of(128 * i)
        low = iota((8, 128), 1) < 64
        turned = pltpu.roll(x, 64, 1)
        for odd in range(2):
            n = 2 * i + odd
            oa_ref[n, 0:CA, :] = wide[CA * n : CA * n + CA, 0:D].astype(BF)
            both = jnp.where(low, turned, x) if odd else jnp.where(low, x, turned)
            oa_ref[n, CA : CA + 8, :] = jnp.zeros((8, D), BF)
            oa_ref[n, CA : CA + 8, 0:128] = both.astype(BF)
    for ref, at, size in ((op_ref, OP, CX), (om_ref, OM, CX)):
        ref[0:size, :] = wide[at : at + size, 0:D].astype(BF)
        ref[size : size + 8, :] = jnp.zeros((8, D), BF)
        for k in range((size + 127) // 128):
            ref[size : size + 8, 128 * k : 128 * k + 128] = facts_of(at + 128 * k).astype(BF)


def pack(where, edges, sent, info, slot_row, first):
    sds = jax.ShapeDtypeStruct
    fixed = lambda *shape: pl.BlockSpec(shape, lambda b: (0,) * len(shape))
    shapes = ((NP, CA + 8, D), (CX + 8, D), (CX + 8, D), (N1, D + 128))
    return pl.pallas_call(
        pack_kernel,
        grid=(1,),
        in_specs=[pl.BlockSpec(memory_space=pltpu.SMEM)]
        + [fixed(N1, D), fixed(N1, D), fixed(N1, 128), fixed(8, N1 + 128), fixed(NH, WROWS, D)],
        out_specs=tuple(fixed(*x) for x in shapes),
        out_shape=tuple(sds(x, BF) for x in shapes),
        scratch_shapes=[pltpu.VMEM((OS, D + 128), F32)],
        compiler_params=pltpu.CompilerParams(vmem_limit_bytes=VMEM),
        name="pack",
    )(where, edges, sent, info, slot_row, first)


def full(w_refs):
    return jnp.concatenate([w[...].reshape(D // 2, D) for w in w_refs], axis=0)


def weight_specs(*which):
    one = lambda k: pl.BlockSpec((NH // 2, 64, D), lambda *_: (0, k, 0))
    vec = pl.BlockSpec((NH, 8, D), lambda *_: (0, VROW // 8, 0))
    return [one(k) for k in which for _ in range(2)] + [vec]


def messages(x, l, proj, w_out, vec):
    hit = onehot(iota((x.shape[0], ML), 1).astype(F32) == l)
    hidden = silu(x + dot(hit, proj)).astype(BF)
    message = normalized(dot(hidden, w_out) + vec[0], vec[1], vec[2])
    return jnp.where(l >= 0.0, message, 0.0).astype(BF)


def edge_vectors(v_ref):
    return vectors_of(v_ref, 1) + vectors_of(v_ref, 2)[0:1]


def local_kernel(where_ref, pre_ref, slot_row_ref, mesh_ref, wr_ref, wr2_ref, wo_ref, wo2_ref, v_ref, proj_ref, msg_ref, l_ref):
    proj = dot_nt(mesh_ref[...], full((wr_ref, wr2_ref))).astype(BF)
    proj_ref[...] = proj
    vec = edge_vectors(v_ref)
    w_out = full((wo_ref, wo2_ref))
    T = 128

    def some(i, carry):
        at = pl.ds(pl.multiple_of(T * i, T), T)
        hit = onehot((iota((T, N1), 0) + OS + T * i).astype(F32) == slot_row_ref[0:1, 0:N1])
        x = dot(hit, pre_ref[...])
        l = jnp.where(x[:, D + 2 : D + 3] > 0.5, x[:, D : D + 1] * 256.0 + x[:, D + 1 : D + 2], -1.0)
        msg_ref[at, :] = messages(x[:, 0:D], l, proj_ref[...], w_out, vec)
        l_ref[:, at] = jnp.broadcast_to(l, (T, 128)).T[0:8, :]
        return carry

    lax.fori_loop(0, CS // T, some, 0)


def local(where, pre, slot_row, mesh_latent, weights):
    first, walk, other = weights
    sds = jax.ShapeDtypeStruct
    fixed = lambda *shape: pl.BlockSpec(shape, lambda b, w: (0,) * len(shape))
    return pl.pallas_call(
        local_kernel,
        grid_spec=pltpu.PrefetchScalarGridSpec(
            num_scalar_prefetch=1,
            grid=(1,),
            in_specs=[
                fixed(N1, D + 128), fixed(8, N1 + 128),
                pl.BlockSpec((ML, D), lambda b, w: (w[0], 0)),
            ] + weight_specs(0, 3),
            out_specs=(fixed(ML, D), fixed(CS, D), fixed(8, CS)),
        ),
        out_shape=(sds((ML, D), BF), sds((CS, D), BF), sds((8, CS), F32)),
        compiler_params=pltpu.CompilerParams(vmem_limit_bytes=VMEM),
        name="local",
    )(where, pre, slot_row, mesh_latent, walk, other, walk, other, first)


def owner_kernel(
    ra_ref, rp_ref, rm_ref, proj_ref, wo_ref, wo2_ref, v_ref,
    oa_ref, op_ref, om_ref, l_row_ref, flag_ref,
    x_s, l_col,
):
    low = iota((8, 128), 1) < 64
    flags = jnp.zeros((8, 128), F32)
    pieces = []
    for i in range(NP // 2):
        a = ra_ref[2 * i, CA : CA + 8, 0:128].astype(F32)
        b = ra_ref[2 * i + 1, CA : CA + 8, 0:128].astype(F32)
        pieces.append(jnp.where(low, a, b))
    for ref, size in ((rp_ref, CX), (rm_ref, CX)):
        for k in range((size + 127) // 128):
            pieces.append(ref[size : size + 8, 128 * k : 128 * k + 128].astype(F32))
    for k, m in enumerate(pieces):
        flags = jnp.maximum(flags, m)
        l = jnp.where(m[2:3] > 0.5, m[0:1] * 256.0 + m[1:2], -1.0)
        l = jnp.broadcast_to(l, (8, 128))
        l_row_ref[:, 128 * k : 128 * k + 128] = l
        l_col[128 * k : 128 * k + 128, :] = l.T
    flag_ref[...] = jnp.broadcast_to(flags[3:4], (8, 128))
    for n in range(NP):
        x_s[CA * n : CA * n + CA, :] = ra_ref[n, 0:CA, :]
    for ref, at in ((rp_ref, OP), (rm_ref, OM)):
        x_s[at : at + CX, :] = ref[0:CX, :]
        x_s[at + CX : at + 256, :] = jnp.zeros((256 - CX, D), BF)
    vec = edge_vectors(v_ref)
    w_out = full((wo_ref, wo2_ref))
    T = 384

    def some(i, carry):
        at = pl.ds(pl.multiple_of(T * i, T), T)
        x_s[at, :] = messages(x_s[at, :].astype(F32), l_col[at, 0:1], proj_ref[...], w_out, vec)
        return carry

    lax.fori_loop(0, OS // T, some, 0)
    for n in range(NP):
        oa_ref[n, :, :] = x_s[CA * n : CA * n + CA, :]
    op_ref[...] = x_s[OP : OP + CX, :]
    om_ref[...] = x_s[OM : OM + CX, :]


def owner(ra, rp, rm, proj, weights):
    first, walk, other = weights
    sds = jax.ShapeDtypeStruct
    fixed = lambda *shape: pl.BlockSpec(shape, lambda b: (0,) * len(shape))
    return pl.pallas_call(
        owner_kernel,
        grid=(1,),
        in_specs=[fixed(NP, CA + 8, D), fixed(CX + 8, D), fixed(CX + 8, D), fixed(ML, D)] + weight_specs(3),
        out_specs=(fixed(NP, CA, D), fixed(CX, D), fixed(CX, D), fixed(8, OS), fixed(8, 128)),
        out_shape=(
            sds((NP, CA, D), BF), sds((CX, D), BF), sds((CX, D), BF), sds((8, OS), F32), sds((8, 128), F32),
        ),
        scratch_shapes=[pltpu.VMEM((OS, D), BF), pltpu.VMEM((OS, 8), F32)],
        compiler_params=pltpu.CompilerParams(vmem_limit_bytes=VMEM),
        name="owner",
    )(ra, rp, rm, proj, walk, other, first)


def nodes_kernel(
    where_ref, oa_ref, op_ref, om_ref, own_msg_ref, l_ref, own_l_ref, mesh_ref,
    wi_ref, wi2_ref, wm_ref, wm2_ref, wo_ref, wo2_ref, v_ref,
    out_ref, out_s,
):
    bias = vectors_of(v_ref, 0, walk_of(where_ref[0]))[1:2]
    vec = bias + vectors_of(v_ref, 2)[1:2] + vectors_of(v_ref, 3)
    w_in, w_msg, w_out = full((wi_ref, wi2_ref)), full((wm_ref, wm2_ref)), full((wo_ref, wo2_ref))
    S = ML // 4

    def some(i, carry):
        at = pl.ds(pl.multiple_of(S * i, S), S)
        row = (iota((S, 1), 0) + S * i).astype(F32)
        summed = dot(onehot(row == l_ref[0:1, 0:OP]), oa_ref[...].reshape(OP, D))
        summed += dot(onehot(row == l_ref[0:1, OP : OP + CX]), op_ref[...])
        summed += dot(onehot(row == l_ref[0:1, OM : OM + CX]), om_ref[...])
        summed += dot(onehot(row == own_l_ref[0:1, :]), own_msg_ref[...])
        own = mesh_ref[at, :]
        before = dot_nt(own, w_in) + dot_nt(summed.astype(BF), w_msg) + vec[0]
        hidden = silu(before).astype(BF)
        total = dot(hidden, w_out) + vec[1]
        out_s[at, :] = own.astype(F32) + normalized(total, vec[2], vec[3])
        return carry

    lax.fori_loop(0, 4, some, 0)
    for t in range(ML // 128):
        for k in range(4):
            turned = out_s[128 * t : 128 * t + 128, 128 * k : 128 * k + 128].T.astype(BF)
            out_ref[2 * k, 64 * t : 64 * t + 64, :] = turned[0:64]
            out_ref[2 * k + 1, 64 * t : 64 * t + 64, :] = turned[64:128]


def nodes(where, oa, op, om, own_msg, l_row, own_l, mesh_latent, weights):
    first, walk, other = weights
    sds = jax.ShapeDtypeStruct
    fixed = lambda *shape: pl.BlockSpec(shape, lambda b, w: (0,) * len(shape))
    return pl.pallas_call(
        nodes_kernel,
        grid_spec=pltpu.PrefetchScalarGridSpec(
            num_scalar_prefetch=1,
            grid=(1,),
            in_specs=[
                fixed(NP, CA, D), fixed(CX, D), fixed(CX, D), fixed(CS, D), fixed(8, OS), fixed(8, CS),
                pl.BlockSpec((ML, D), lambda b, w: (w[0], 0)),
            ] + weight_specs(1, 2, 4),
            out_specs=fixed(NH, ML // 2, 128),
            scratch_shapes=[pltpu.VMEM((ML, D), F32)],
        ),
        out_shape=sds((NH, ML // 2, 128), BF),
        compiler_params=pltpu.CompilerParams(vmem_limit_bytes=VMEM),
        name="nodes",
    )(where, oa, op, om, own_msg, l_row, own_l, mesh_latent, walk, other, walk, other, walk, other, first)


def unpack_kernel(ma_ref, mp_ref, mm_ref, ms_ref, slot_ref, flag_ref, mesh_ref, out_ref, msg, rows):
    for n in range(NP):
        msg[CA * n : CA * n + CA, :] = ma_ref[n]
    for ref, at in ((mp_ref, OP), (mm_ref, OM)):
        msg[at : at + CX, :] = ref[...]
        msg[at + CX : at + 256, :] = jnp.zeros((256 - CX, D), BF)
    msg[OS : OS + CS, :] = ms_ref[...]
    T = 384

    def one(i, carry):
        at = pl.ds(pl.multiple_of(T * i, T), T)
        hit = onehot(iota((T, NS), 1).astype(F32) == slot_ref[at, 0:1])
        rows[at, :] = dot(hit, msg[...])
        return carry

    lax.fori_loop(0, N1 // T, one, 0)
    for k in range(NH // 2):
        at = slice(128 * k, 128 * k + 128)
        a, b = lane_join(rows[0:HALF, at], rows[HALF:N1, at])
        out_ref[2 * k, 0:HALF, :] = a.astype(BF)
        out_ref[2 * k + 1, 0:HALF, :] = b.astype(BF)
    flag = jnp.concatenate([flag_ref[...]] * (FLAG // 8), axis=0).astype(BF)
    for n in range(NH):
        out_ref[n, HALF:MESH_AT, :] = flag
        out_ref[n, MESH_AT:OUT_ROWS, :] = mesh_ref[n]


def unpack(ma, mp, mm, ms, slots, flag, mesh_blocks):
    return pl.pallas_call(
        unpack_kernel,
        out_shape=jax.ShapeDtypeStruct((NH, OUT_ROWS, 128), BF),
        scratch_shapes=[pltpu.VMEM((NS, D), BF), pltpu.VMEM((N1, D), F32)],
        compiler_params=pltpu.CompilerParams(vmem_limit_bytes=VMEM),
        name="unpack",
    )(ma, mp, mm, ms, slots, flag, mesh_blocks)


def columns_kernel(where_ref, edge_ref, out_ref):
    odd = (where_ref[0] & 1) == 1
    low = iota((128, 128), 1) < 64
    for i in range(8):
        a = edge_ref[256 * i : 256 * i + 128, :].astype(F32)
        b = edge_ref[256 * i + 128 : 256 * i + 256, :].astype(F32)
        left, right = jnp.where(low, a, pltpu.roll(b, 64, 1)), jnp.where(low, pltpu.roll(a, 64, 1), b)
        turned = jnp.where(odd, right, left).T.astype(BF)
        out_ref[:, 256 * i : 256 * i + 128] = turned[0:64]
        out_ref[:, 256 * i + 128 : 256 * i + 256] = turned[64:128]


def columns(where, edge_latent):
    return pl.pallas_call(
        columns_kernel,
        grid_spec=pltpu.PrefetchScalarGridSpec(
            num_scalar_prefetch=1,
            grid=(4,),
            in_specs=[pl.BlockSpec((E // 4, 128), lambda b, w: (b, w[0] // 2))],
            out_specs=pl.BlockSpec((64, E // 4), lambda b, w: (0, b)),
        ),
        out_shape=jax.ShapeDtypeStruct((64, E), BF),
        compiler_params=pltpu.CompilerParams(vmem_limit_bytes=VMEM),
        name="columns",
    )(where, edge_latent)


def finish_kernel(starts_ref, in_ref, key_ref, column_ref, out_ref, mesh_ref, flag_ref, lists):
    flag = jnp.zeros((8, 128), F32)
    half = iota((HALF, 128), 1) < 64
    for n in range(NH):
        x = in_ref[n, 0:HALF, :].astype(F32)
        turned = pltpu.roll(x, 64, 1)
        lists[n, 0:HALF, :] = jnp.where(half, x, turned).astype(BF)
        lists[n, HALF:N1, :] = jnp.where(half, turned, x).astype(BF)
        lists[n, N1 : N1 + WIN, :] = jnp.zeros((WIN, 128), BF)
        flag = jnp.maximum(flag, in_ref[n, HALF : HALF + 8, :].astype(F32))
        for t in range(ML // 128):
            at = ML * n + 128 * t
            mesh_ref[:, at : at + 128] = in_ref[n, MESH_AT + 64 * t : MESH_AT + 64 * t + 64, :]
    flag_ref[0, 0] = (jnp.max(flag) > 0.5).astype(I32)
    low = iota((128, 128), 1) < 64
    lane = iota((128, NH * WIN), 1).astype(F32)

    def group(g, carry):
        key = key_ref[pl.ds(pl.multiple_of(8 * g, 8), 8), :]
        h = jnp.floor(key * (1.0 / 256.0))
        delta = key - 256.0 * h
        column = jnp.where((h >= 0.0) & (delta < WIN), h * WIN + delta, -1.0).T
        for i in range(4):
            sides = []
            for j in (2 * i, 2 * i + 1):
                hit = onehot(lane == column[:, j : j + 1])
                parts = []
                for n in range(NH):
                    at = jnp.minimum(starts_ref[8 * g + j, n], N1)
                    parts.append(lists[n, pl.ds(pl.multiple_of(at, 16), WIN), :])
                sides.append(dot(hit, jnp.concatenate(parts, axis=0)))
            turned = jnp.where(low, sides[0], sides[1]).T
            for k in range(2):
                at = pl.ds(pl.multiple_of(1024 * g + 256 * i + 128 * k, 128), 128)
                out_ref[:, at] = (turned[64 * k : 64 * k + 64] + column_ref[:, at].astype(F32)).astype(BF)
        return carry

    lax.fori_loop(0, 8, group, 0)


def finish(starts, lists, key, column):
    sds = jax.ShapeDtypeStruct
    smem = pl.BlockSpec(memory_space=pltpu.SMEM)
    vmem = pl.BlockSpec(memory_space=pltpu.VMEM)
    return pl.pallas_call(
        finish_kernel,
        in_specs=[smem, vmem, vmem, vmem],
        out_specs=(vmem, vmem, smem),
        out_shape=(sds((64, E), BF), sds((64, M), BF), sds((1, 1), I32)),
        scratch_shapes=[pltpu.VMEM((NH, N1 + WIN, 128), BF)],
        compiler_params=pltpu.CompilerParams(vmem_limit_bytes=VMEM),
        name="finish",
    )(starts, lists, key, column)


def exchange(a, p, m, away):
    up = [(i, (i + 1) % NP) for i in range(NP)]
    down = [(i, (i - 1) % NP) for i in range(NP)]
    first, second = (up, down) if away else (down, up)
    p = lax.ppermute(p, "patch", first)
    m = lax.ppermute(m, "patch", second)
    a = lax.all_to_all(a, "patch", split_axis=0, concat_axis=0, tiled=True)
    return a, p, m


def fast(
    grid_latent, mesh_latent, edge_latent, senders, receivers, mesh_slot, edge_counts,
    w_edge, w_sender, w_receiver, edge_bias, w_edge_out, edge_out_bias, edge_gain, edge_shift,
    w_mesh_in, w_message_in, mesh_bias, w_mesh_out, mesh_out_bias, mesh_gain, mesh_shift,
):
    patch = lax.axis_index("patch").astype(I32)
    own = lax.axis_index("hidden").astype(I32)
    where = jnp.stack([own, patch])
    vectors = (edge_bias, mesh_bias, edge_out_bias, edge_gain, edge_shift, mesh_out_bias, mesh_gain, mesh_shift)
    first, second = stacked(
        w_edge.T, w_sender.T, w_receiver.T, w_mesh_in.T, w_message_in.T, w_edge_out, w_mesh_out,
        *(v.reshape(1, 64) for v in vectors),
    )
    weights = to_all(first, second)
    key, starts, edges, sent, info, slots, slot_row, target = gather(
        edge_counts, where, receivers, mesh_slot, senders, edge_latent, grid_latent
    )
    sa, sp, sm, pre = pack(where, edges, sent, info, slot_row, weights[0])
    ra, rp, rm = exchange(sa, sp, sm, True)
    proj, ms, own_l = local(where, pre, slot_row, mesh_latent, weights)
    column = columns(where, edge_latent)
    oa, op, om, l_row, flag = owner(ra, rp, rm, proj, weights)
    ma, mp, mm = exchange(oa, op, om, False)
    mesh_blocks = nodes(where, oa, op, om, ms, l_row, own_l, mesh_latent, weights)
    lists = unpack(ma, mp, mm, ms, slots, flag, mesh_blocks)
    lists = lax.all_to_all(lists, "hidden", split_axis=0, concat_axis=0, tiled=True)
    edge_out, mesh_out, flag = finish(starts, lists, key, column)
    return mesh_out.T, edge_out.T, flag, target


def from_everyone(x):
    copies = jnp.broadcast_to(x, (NH, *x.shape))
    return lax.all_to_all(copies, "hidden", split_axis=0, concat_axis=0, tiled=True)


def by_rows(f, size, *xs):
    part = lambda x, i: lax.dynamic_slice_in_dim(x, size * i, size)
    shape = jax.eval_shape(f, *(jax.ShapeDtypeStruct((size, *x.shape[1:]), x.dtype) for x in xs))
    out = jnp.zeros((xs[0].shape[0], *shape.shape[1:]), shape.dtype)

    def one(i, out):
        return lax.dynamic_update_slice_in_dim(out, f(*(part(x, i) for x in xs)), size * i, 0)

    return lax.fori_loop(0, xs[0].shape[0] // size, one, out)


def times(x, w):
    return by_rows(lambda y: dot(y, w), 128, x)


def rows_at(table, index):
    ids = jnp.arange(table.shape[0], dtype=I32)
    return by_rows(lambda at: dot((at[:, None] == ids[None, :]).astype(BF), table), 128, index)


def sums_at(rows, index):
    def some(ids):
        def one(i, out):
            at = lax.dynamic_slice_in_dim(index, 512 * i, 512)
            return out + dot((ids[:, None] == at[None, :]).astype(BF), lax.dynamic_slice_in_dim(rows, 512 * i, 512))

        return lax.fori_loop(0, E // 512, one, jnp.zeros((ids.shape[0], rows.shape[1]), F32))

    return by_rows(some, 128, jnp.arange(M, dtype=I32))


def second_layer(pre, w):
    partial = by_rows(lambda x: dot(silu(x).astype(BF), w).astype(BF), 128, pre)
    blocks = lax.all_to_all(jnp.stack(jnp.split(partial, NH, axis=1)), "hidden", split_axis=0, concat_axis=0, tiled=True)
    return by_rows(lambda *x: sum(y.astype(F32) for y in x), 128, *blocks)


def finished(v, gain, shift, scale, columns):
    parts = by_rows(lambda x: jnp.stack([jnp.sum(x, axis=1), jnp.sum(x * x, axis=1)], axis=1), 128, v)
    total = from_everyone(parts.T).sum(axis=0).T / D

    def one(x, t, scale):
        var = jnp.maximum(t[:, 1:2] - t[:, 0:1] * t[:, 0:1], 0.0)
        return ((x - t[:, 0:1]) * lax.rsqrt(var + EPSILON) * gain + shift) * scale

    change = by_rows(one, 128, v, total, scale)
    return by_rows(lambda c, x: (c.astype(F32) + x).astype(BF), 128, columns, change), change


def slow(
    target,
    grid_latent, mesh_latent, edge_latent, senders, receivers, mesh_slot, edge_counts,
    w_edge, w_sender, w_receiver, edge_bias, w_edge_out, edge_out_bias, edge_gain, edge_shift,
    w_mesh_in, w_message_in, mesh_bias, w_mesh_out, mesh_out_bias, mesh_gain, mesh_shift,
):
    patch = lax.axis_index("patch").astype(I32)
    own = lax.axis_index("hidden").astype(I32)
    up = [(i, (i + 1) % NP) for i in range(NP)]
    target = target.astype(I32).reshape(E)
    whose = target // M
    local = target - whose * M
    live = (jnp.arange(E, dtype=I32) < edge_counts[0]).astype(F32)
    sent = rows_at(grid_latent, senders - patch * G).astype(BF)
    pre = times(edge_latent, w_edge) + times(sent, w_sender) + edge_bias

    def fetch(s, state):
        block, pre = state
        pre = pre + rows_at(block, jnp.where(whose == (patch - s) % NP, local, -1))
        return lax.ppermute(block, "patch", up), pre

    block = times(mesh_latent, w_receiver).astype(BF)
    _, pre = lax.fori_loop(0, NP, fetch, (block, pre))
    total = second_layer(pre, w_edge_out) + edge_out_bias
    columns = lax.dynamic_slice_in_dim(edge_latent, own * 64, 64, 1)
    edge_out, message = finished(total, edge_gain, edge_shift, live[:, None], columns)
    rows = message.astype(BF)

    def collect(s, sums):
        part = sums_at(rows, jnp.where(whose == (patch - 1 - s) % NP, local, -1))
        return lax.ppermute(sums, "patch", up) + part

    sums = lax.fori_loop(0, NP, collect, jnp.zeros((M, 64), F32))
    summed = jnp.concatenate(list(from_everyone(sums.astype(BF))), axis=1)
    before = times(mesh_latent, w_mesh_in) + times(summed, w_message_in) + mesh_bias
    total = second_layer(before, w_mesh_out) + mesh_out_bias
    columns = lax.dynamic_slice_in_dim(mesh_latent, own * 64, 64, 1)
    mesh_out, _ = finished(total, mesh_gain, mesh_shift, jnp.ones((M, 1), F32), columns)
    return mesh_out, edge_out


def shards(*args):
    mesh_out, edge_out, flag, target = fast(*args)
    return lax.cond(
        flag[0, 0] > 0, lambda a, done: slow(*a), lambda a, done: done, (target, *args), (mesh_out, edge_out)
    )


def solution(mesh):
    rows, columns, units = P("patch", None), P(None, "hidden"), P("hidden")
    return jax.shard_map(
        shards,
        mesh=mesh,
        in_specs=(
            rows, rows, rows, P("patch"), P("patch"), P(), P("patch"),
            columns, columns, columns, units, P("hidden", None), units, units, units,
            columns, columns, units, P("hidden", None), units, units, units,
        ),
        out_specs=(P("patch", "hidden"), P("patch", "hidden")),
        check_vma=False,
    )
```

profile of v0, /device:TPU:1, one launch (start us, length us, event | category | flops | bytes accessed | tf_op | source)
XLA Modules:
  0.0 185.3 jit_solution(11028027905581054478)
XLA Ops:
  0.7 2.5 %stacked.1 = (bf16[8,136,512]{2,1,0:T(8,128)(2,1)}, bf16[320,512]{1,0:T(8,128)(2,1)}) custom-call(bf16[64,512]{1,0:T(8,128)(2,1)} %bitcast.205, bf16[64,512]{1,0:T(8,128)(2,1)} %bitcast.206, bf16[64,512]{1,0:T(8,128)(2,1)} %bitcast.207, bf16[64,512]{1,0:T(8,128)(2,1)} %bitcast.208, bf16[64,512]{1,0:T(8,128)(2,1)} %bitcast.209, bf16[64,512]{1,0:T(8,128)(2,1)} %eo.1, ...), custom_call_target="tpu_custom_call" | custom-call | tf_op jit(solution)/shard_map/stacked/pallas_call | solution.py:298
  3.1 5.8 %all-to-all-start.5 = ((bf16[8,136,512]{2,1,0:T(8,128)(2,1)}), bf16[8,136,512]{2,1,0:T(8,128)(2,1)}, u32[]{:S(2)}, u32[]{:S(2)}) async-start(bf16[8,136,512]{2,1,0:T(8,128)(2,1)} %get-tuple-element.2240), calls=%async_computation.5 | async-start | bytes 2228224 | tf_op jit(solution)/shard_map/all_to_all | solution.py:306
  8.9 1.4 collective-permute-start.4
  10.3 2.4 %collective-permute-start.5 = (bf16[320,512]{1,0:T(8,128)(2,1)}, bf16[320,512]{1,0:T(8,128)(2,1)S(1)}, u32[]{:S(2)}, u32[]{:S(2)}) collective-permute-start(bf16[320,512]{1,0:T(8,128)(2,1)} %get-tuple-element.2245), channel_id=1, source_target_pairs={{0,4},{1,5},{2,6},{3,7},{4,0},{5,1},{6,2},{7,3},{8,12},{9,13},{10,... | collective-permute-start | bytes 983048 | tf_op jit(solution)/shard_map/ppermute | solution.py:309
  13.9 17.7 %collective-permute-done.4 = bf16[320,512]{1,0:T(8,128)(2,1)S(1)} collective-permute-done((bf16[320,512]{1,0:T(8,128)(2,1)}, bf16[320,512]{1,0:T(8,128)(2,1)S(1)}, u32[]{:S(2)}, u32[]{:S(2)}) %collective-permute-start.4) | collective-permute-done | bytes 327712 | tf_op jit(solution)/shard_map/ppermute | solution.py:309
  31.5 7.2 %collective-permute-done.5 = bf16[320,512]{1,0:T(8,128)(2,1)S(1)} collective-permute-done((bf16[320,512]{1,0:T(8,128)(2,1)}, bf16[320,512]{1,0:T(8,128)(2,1)S(1)}, u32[]{:S(2)}, u32[]{:S(2)}) %collective-permute-start.5) | collective-permute-done | bytes 327712 | tf_op jit(solution)/shard_map/ppermute | solution.py:309
  38.7 2.2 %pad_maximum_fusion.wr_ref.wo_ref.wi_ref.wm_ref = bf16[4,320,512]{2,1,0:T(8,128)(2,1)} fusion(bf16[1,320,512]{2,1,0:T(8,128)(2,1)S(1)} %bitcast.204, bf16[1,320,512]{2,1,0:T(8,128)(2,1)S(1)} %bitcast.203, bf16[1,320,512]{2,1,0:T(8,128)(2,1)S(1)} %bitcast.202, bf16[1,320,512]{2,1,0:T(8,128)(2,1)} %bitcast.201), kind=kLoop, calls=%fused_computation.151 | loop fusion | flops 1966080 | bytes 2621440 | tf_op jit(solution)/shard_map/stack | solution.py:310
  43.1 23.9 %gather.1 = (f32[64,128]{1,0:T(8,128)}, s32[72,128]{1,0:T(8,128)}, bf16[1152,512]{1,0:T(8,128)(2,1)}, bf16[1152,512]{1,0:T(8,128)(2,1)}, bf16[1152,128]{1,0:T(8,...) custom-call(s32[1]{0:T(128)S(6)} %copy.458.count_ref, s32[2]{0:T(128)} %pad_add_fusion.where_ref, ...), custom_call_target="tpu_custom_call" | custom-call | tf_op jit(solution)/shard_map/gather/pallas_call | solution.py:233
  67.0 9.6 %pack.1 = (bf16[16,72,512]{2,1,0:T(8,128)(2,1)}, bf16[168,512]{1,0:T(8,128)(2,1)}, bf16[168,512]{1,0:T(8,128)(2,1)}, bf16[1152,640]{1,0:T(8,128)(2,1)}) custom-call(s32[2]{0:T(128)} %pad_add_fusion.where_ref, bf16[1152,512]{1,0:T(8,128)(2,1)} %get-tuple-element.2236.list_ref, bf16[1152,512]{1,0:T(8,128)(2,1)} %get-tuple-element.2237.sent_ref, ...), custom_call_target="tpu_custom_call" | custom-call | tf_op jit(solution)/shard_map/pack/pallas_call | solution.py:363
  76.6 7.8 %all-to-all-start.6 = ((bf16[16,72,512]{2,1,0:T(8,128)(2,1)}), bf16[16,72,512]{2,1,0:T(8,128)(2,1)}, u32[]{:S(2)}, u32[]{:S(2)}) async-start(bf16[16,72,512]{2,1,0:T(8,128)(2,1)} %get-tuple-element.2241), calls=%async_computation.6 | async-start | bytes 2359296 | tf_op jit(solution)/shard_map/all_to_all | solution.py:677
  85.7 3.5 %collective-permute-start.3 = (bf16[168,512]{1,0:T(8,128)(2,1)}, bf16[168,512]{1,0:T(8,128)(2,1)S(1)}, u32[]{:S(2)}, u32[]{:S(2)}) collective-permute-start(bf16[168,512]{1,0:T(8,128)(2,1)} %get-tuple-element.2243), channel_id=1, source_target_pairs={{0,120},{8,0},{16,8},{24,16},{32,24},{40,32},{48,40},{56,48},{64,5... | collective-permute-start | bytes 516104 | tf_op jit(solution)/shard_map/ppermute | solution.py:676
  89.3 7.5 %local.1 = (bf16[640,512]{1,0:T(8,128)(2,1)}, bf16[384,512]{1,0:T(8,128)(2,1)}, f32[8,384]{1,0:T(8,128)}) custom-call(s32[2]{0:T(128)} %pad_add_fusion.where_ref, bf16[1152,640]{1,0:T(8,128)(2,1)} %get-tuple-element.2244.pre_ref, f32[8,1280]{1,0:T(8,128)} %get-tuple-element.2239.slot_row_ref, bf16[5120,512]{1,0:T(8,128)(2,1)} %mesh_ref.3, ...), custom_call_target="tpu_custom_call" | custom-call | tf_op jit(solution)/shard_map/local/pallas_call | solution.py:420
  96.8 9.6 %collective-permute-done.2.rp_ref = bf16[168,512]{1,0:T(8,128)(2,1)S(1)} collective-permute-done((bf16[168,512]{1,0:T(8,128)(2,1)}, bf16[168,512]{1,0:T(8,128)(2,1)S(1)}, u32[]{:S(2)}, u32[]{:S(2)}) %collective-permute-start.2) | collective-permute-done | bytes 172064 | tf_op jit(solution)/shard_map/ppermute | solution.py:675
  107.2 7.7 %owner.1 = (bf16[16,64,512]{2,1,0:T(8,128)(2,1)}, bf16[160,512]{1,0:T(8,128)(2,1)}, bf16[160,512]{1,0:T(8,128)(2,1)}, f32[8,1536]{1,0:T(8,128)}, f32[8,128]{1,0:T(8,128)}) custom-call(bf16[16,72,512]{2,1,0:T(8,128)(2,1)} %all-to-all-done.6.ra_ref, bf16[168,512]{1,0:T(8,128)(2,1)} %copy-done.12, bf16[168,512]{1,0:T(8,128)(2,1)} %copy-done.13, ...), custom_call_target="tpu_custom_call" | custom-call | tf_op jit(solution)/shard_map/owner/pallas_call | solution.py:484
  114.8 4.3 %all-to-all-start.7 = ((bf16[16,64,512]{2,1,0:T(8,128)(2,1)}), bf16[16,64,512]{2,1,0:T(8,128)(2,1)}, u32[]{:S(2)}, u32[]{:S(2)}) async-start(bf16[16,64,512]{2,1,0:T(8,128)(2,1)} %get-tuple-element.2247.oa_ref), calls=%async_computation.7 | async-start | bytes 2097152 | tf_op jit(solution)/shard_map/all_to_all | solution.py:677
  119.2 4.6 %collective-permute-start.8 = (bf16[160,512]{1,0:T(8,128)(2,1)}, bf16[160,512]{1,0:T(8,128)(2,1)S(1)}, u32[]{:S(2)}, u32[]{:S(2)}) collective-permute-start(bf16[160,512]{1,0:T(8,128)(2,1)} %get-tuple-element.2248.op_ref), channel_id=1, source_target_pairs={{0,120},{8,0},{16,8},{24,16},{32,24},{40,32},{48,40},{56,48},{64,5... | collective-permute-start | bytes 491528 | tf_op jit(solution)/shard_map/ppermute | solution.py:675
  123.8 9.4 %nodes.1.mesh_ref = bf16[8,320,128]{2,1,0:T(8,128)(2,1)} custom-call(s32[2]{0:T(128)} %pad_add_fusion.where_ref, bf16[16,64,512]{2,1,0:T(8,128)(2,1)} %get-tuple-element.2247.oa_ref, bf16[160,512]{1,0:T(8,128)(2,1)} %get-tuple-element.2248.op_ref, bf16[160,512]{1,0:T(8,128)(2,1)} %get-tuple-element.2249.om_ref, ...), custom_call_target="tpu_custom_call" | custom-call | tf_op jit(solution)/shard_map/nodes/pallas_call | solution.py:534
  133.2 1.8 collective-permute-done.8.mp_ref
  135.0 3.9 %collective-permute-done.9.mm_ref = bf16[160,512]{1,0:T(8,128)(2,1)S(1)} collective-permute-done((bf16[160,512]{1,0:T(8,128)(2,1)}, bf16[160,512]{1,0:T(8,128)(2,1)S(1)}, u32[]{:S(2)}, u32[]{:S(2)}) %collective-permute-start.9) | collective-permute-done | bytes 163872 | tf_op jit(solution)/shard_map/ppermute | solution.py:676
  139.6 6.7 %unpack.1 = bf16[8,912,128]{2,1,0:T(8,128)(2,1)} custom-call(bf16[16,64,512]{2,1,0:T(8,128)(2,1)} %all-to-all-done.7.ma_ref, bf16[160,512]{1,0:T(8,128)(2,1)} %copy-done.14, bf16[160,512]{1,0:T(8,128)(2,1)} %copy-done.15, bf16[384,512]{1,0:T(8,128)(2,1)} %get-tuple-element.2250.own_msg_ref.ms_ref, f32[1152,8]{1,0:T(8,128)} %get-tuple-element.2251.slot_ref, ...), custom_call_target="tpu_custom_call" | custom-call | tf_op jit(solution)/shard_map/unpack/pallas_call | solution.py:580
  146.2 5.7 %all-to-all-start.8 = ((bf16[8,912,128]{2,1,0:T(8,128)(2,1)}), bf16[8,912,128]{2,1,0:T(8,128)(2,1)}, u32[]{:S(2)}, u32[]{:S(2)}) async-start(bf16[8,912,128]{2,1,0:T(8,128)(2,1)} %unpack.1), calls=%async_computation.8 | async-start | bytes 3735552 | tf_op jit(solution)/shard_map/all_to_all | solution.py:706
  152.0 5.2 %columns.1.column_ref = bf16[64,8192]{1,0:T(8,128)(2,1)} custom-call(s32[2]{0:T(128)} %pad_add_fusion.where_ref, bf16[8192,512]{1,0:T(8,128)(2,1)} %edge_ref.1), custom_call_target="tpu_custom_call" | custom-call | tf_op jit(solution)/shard_map/columns/pallas_call | solution.py:602
  157.2 18.6 %all-to-all-done.8.in_ref = bf16[8,912,128]{2,1,0:T(8,128)(2,1)} async-done(((bf16[8,912,128]{2,1,0:T(8,128)(2,1)}), bf16[8,912,128]{2,1,0:T(8,128)(2,1)}, u32[]{:S(2)}, u32[]{:S(2)}) %all-to-all-start.8) | async-done | bytes 1867808 | tf_op jit(solution)/shard_map/all_to_all | solution.py:706
  175.9 8.6 %finish.1 = (bf16[64,8192]{1,0:T(8,128)(2,1)}, bf16[64,5120]{1,0:T(8,128)(2,1)}, s32[1,1]{1,0:T(1,128)}) custom-call(s32[72,128]{1,0:T(8,128)} %get-tuple-element.2235.starts_ref, bf16[8,912,128]{2,1,0:T(8,128)(2,1)} %all-to-all-done.8.in_ref, f32[64,128]{1,0:T(8,128)} %get-tuple-element.2255.key_ref, bf16[64,8192]{1,0:T(8,128)(2,1)} %columns.1.column_ref), custom_call_target="tpu_custom_call" | custom-call | tf_op jit(solution)/shard_map/finish/pallas_call | solution.py:660
  (38 shorter events, 5.6 us)
Async XLA Ops:
  0.6 42.5 %copy-start.16 = (s32[8192]{0:T(1024)S(1)}, s32[8192]{0:T(1024)}, u32[]{:S(2)}) copy-start(s32[8192]{0:T(1024)} %param.69) | copy-start | bytes 98308
  0.6 42.5 %copy-start = (bf16[3072,512]{1,0:T(8,128)(2,1)S(1)}, bf16[3072,512]{1,0:T(8,128)(2,1)}, u32[]{:S(2)}) copy-start(bf16[3072,512]{1,0:T(8,128)(2,1)} %grid_hbm.1) | copy-start | bytes 9437188
  3.1 63.9 %all-to-all-start.5 = ((bf16[8,136,512]{2,1,0:T(8,128)(2,1)}), bf16[8,136,512]{2,1,0:T(8,128)(2,1)}, u32[]{:S(2)}, u32[]{:S(2)}) async-start(bf16[8,136,512]{2,1,0:T(8,128)(2,1)} %get-tuple-element.2240), calls=%async_computation.5 | async-start | bytes 2228224 | tf_op jit(solution)/shard_map/all_to_all | solution.py:306
  8.9 22.6 %collective-permute-start.4 = (bf16[320,512]{1,0:T(8,128)(2,1)}, bf16[320,512]{1,0:T(8,128)(2,1)S(1)}, u32[]{:S(2)}, u32[]{:S(2)}) collective-permute-start(bf16[320,512]{1,0:T(8,128)(2,1)} %get-tuple-element.2245), channel_id=1, source_target_pairs={{0,2},{1,3},{2,4},{3,5},{4,6},{5,7},{6,0},{7,1},{8,10},{9,11},{10,... | collective-permute-start | bytes 983048 | tf_op jit(solution)/shard_map/ppermute | solution.py:309
  10.3 28.4 %collective-permute-start.5 = (bf16[320,512]{1,0:T(8,128)(2,1)}, bf16[320,512]{1,0:T(8,128)(2,1)S(1)}, u32[]{:S(2)}, u32[]{:S(2)}) collective-permute-start(bf16[320,512]{1,0:T(8,128)(2,1)} %get-tuple-element.2245), channel_id=1, source_target_pairs={{0,4},{1,5},{2,6},{3,7},{4,0},{5,1},{6,2},{7,3},{8,12},{9,13},{10,... | collective-permute-start | bytes 983048 | tf_op jit(solution)/shard_map/ppermute | solution.py:309
  12.7 26.0 %collective-permute-start.6 = (bf16[320,512]{1,0:T(8,128)(2,1)}, bf16[320,512]{1,0:T(8,128)(2,1)S(1)}, u32[]{:S(2)}, u32[]{:S(2)}) collective-permute-start(bf16[320,512]{1,0:T(8,128)(2,1)} %get-tuple-element.2245), channel_id=1, source_target_pairs={{0,6},{1,7},{2,0},{3,1},{4,2},{5,3},{6,4},{7,5},{8,14},{9,15},{10,... | collective-permute-start | bytes 983048 | tf_op jit(solution)/shard_map/ppermute | solution.py:309
  40.9 48.4 %collective-permute-start.7 = (bf16[4,320,512]{2,1,0:T(8,128)(2,1)}, bf16[4,320,512]{2,1,0:T(8,128)(2,1)}, u32[]{:S(2)}, u32[]{:S(2)}) collective-permute-start(bf16[4,320,512]{2,1,0:T(8,128)(2,1)} %pad_maximum_fusion.wr_ref.wo_ref.wi_ref.wm_ref), channel_id=1, source_target_pairs={{0,1},{1,0},{2,3},{3,2},{4,5},{5,4},{6,7},{7,6},{8,9},{9,8},{10,11... | collective-permute-start | bytes 3932168 | tf_op jit(solution)/shard_map/ppermute | solution.py:311
  76.6 29.9 %all-to-all-start.6 = ((bf16[16,72,512]{2,1,0:T(8,128)(2,1)}), bf16[16,72,512]{2,1,0:T(8,128)(2,1)}, u32[]{:S(2)}, u32[]{:S(2)}) async-start(bf16[16,72,512]{2,1,0:T(8,128)(2,1)} %get-tuple-element.2241), calls=%async_computation.6 | async-start | bytes 2359296 | tf_op jit(solution)/shard_map/all_to_all | solution.py:677
  84.4 22.0 %collective-permute-start.2 = (bf16[168,512]{1,0:T(8,128)(2,1)}, bf16[168,512]{1,0:T(8,128)(2,1)S(1)}, u32[]{:S(2)}, u32[]{:S(2)}) collective-permute-start(bf16[168,512]{1,0:T(8,128)(2,1)} %get-tuple-element.2242), channel_id=1, source_target_pairs={{0,8},{8,16},{16,24},{24,32},{32,40},{40,48},{48,56},{56,64},{64,7... | collective-permute-start | bytes 516104 | tf_op jit(solution)/shard_map/ppermute | solution.py:675
  85.7 20.7 %collective-permute-start.3 = (bf16[168,512]{1,0:T(8,128)(2,1)}, bf16[168,512]{1,0:T(8,128)(2,1)S(1)}, u32[]{:S(2)}, u32[]{:S(2)}) collective-permute-start(bf16[168,512]{1,0:T(8,128)(2,1)} %get-tuple-element.2243), channel_id=1, source_target_pairs={{0,120},{8,0},{16,8},{24,16},{32,24},{40,32},{48,40},{56,48},{64,5... | collective-permute-start | bytes 516104 | tf_op jit(solution)/shard_map/ppermute | solution.py:676
  106.4 0.8 copy-start.13
  114.8 24.1 %all-to-all-start.7 = ((bf16[16,64,512]{2,1,0:T(8,128)(2,1)}), bf16[16,64,512]{2,1,0:T(8,128)(2,1)}, u32[]{:S(2)}, u32[]{:S(2)}) async-start(bf16[16,64,512]{2,1,0:T(8,128)(2,1)} %get-tuple-element.2247.oa_ref), calls=%async_computation.7 | async-start | bytes 2097152 | tf_op jit(solution)/shard_map/all_to_all | solution.py:677
  119.2 15.8 %collective-permute-start.8 = (bf16[160,512]{1,0:T(8,128)(2,1)}, bf16[160,512]{1,0:T(8,128)(2,1)S(1)}, u32[]{:S(2)}, u32[]{:S(2)}) collective-permute-start(bf16[160,512]{1,0:T(8,128)(2,1)} %get-tuple-element.2248.op_ref), channel_id=1, source_target_pairs={{0,120},{8,0},{16,8},{24,16},{32,24},{40,32},{48,40},{56,48},{64,5... | collective-permute-start | bytes 491528 | tf_op jit(solution)/shard_map/ppermute | solution.py:675
  123.8 15.1 %collective-permute-start.9 = (bf16[160,512]{1,0:T(8,128)(2,1)}, bf16[160,512]{1,0:T(8,128)(2,1)S(1)}, u32[]{:S(2)}, u32[]{:S(2)}) collective-permute-start(bf16[160,512]{1,0:T(8,128)(2,1)} %get-tuple-element.2249.om_ref), channel_id=1, source_target_pairs={{0,8},{8,16},{16,24},{24,32},{32,40},{40,48},{48,56},{56,64},{64,7... | collective-permute-start | bytes 491528 | tf_op jit(solution)/shard_map/ppermute | solution.py:676
  135.0 3.9 %copy-start.14 = (bf16[160,512]{1,0:T(8,128)(2,1)}, bf16[160,512]{1,0:T(8,128)(2,1)S(1)}, u32[]{:S(2)}) copy-start(bf16[160,512]{1,0:T(8,128)(2,1)S(1)} %collective-permute-done.8.mp_ref) | copy-start | bytes 491524
  138.9 0.7 copy-start.15
  146.2 29.6 %all-to-all-start.8 = ((bf16[8,912,128]{2,1,0:T(8,128)(2,1)}), bf16[8,912,128]{2,1,0:T(8,128)(2,1)}, u32[]{:S(2)}, u32[]{:S(2)}) async-start(bf16[8,912,128]{2,1,0:T(8,128)(2,1)} %unpack.1), calls=%async_computation.8 | async-start | bytes 3735552 | tf_op jit(solution)/shard_map/all_to_all | solution.py:706
  152.0 33.1 %copy-start.8 = (bf16[512,64]{0,1:T(8,128)(2,1)S(1)}, bf16[512,64]{0,1:T(8,128)(2,1)}, u32[]{:S(2)}) copy-start(bf16[512,64]{0,1:T(8,128)(2,1)} %param.73) | copy-start | bytes 196612
  152.0 33.1 %copy-start.17 = (s32[8192]{0:T(1024)S(1)}, s32[8192]{0:T(1024)}, u32[]{:S(2)}) copy-start(s32[8192]{0:T(1024)} %param.69) | copy-start | bytes 98308
  152.0 33.1 %copy-start.20 = (f32[64,128]{1,0:T(8,128)S(1)}, f32[64,128]{1,0:T(8,128)}, u32[]{:S(2)}) copy-start(f32[64,128]{1,0:T(8,128)} %get-tuple-element.2259) | copy-start | bytes 98308
  152.0 33.1 %copy-start.21 = (f32[64]{0:T(128)S(1)}, f32[64]{0:T(128)}, u32[]{:S(2)}) copy-start(f32[64]{0:T(128)} %param.79) | copy-start | bytes 772
  152.0 33.1 %copy-start.22 = (f32[64]{0:T(128)S(1)}, f32[64]{0:T(128)}, u32[]{:S(2)}) copy-start(f32[64]{0:T(128)} %param.80) | copy-start | bytes 772
  152.0 33.1 %copy-start.25 = (f32[64]{0:T(128)S(1)}, f32[64]{0:T(128)}, u32[]{:S(2)}) copy-start(f32[64]{0:T(128)} %param.76) | copy-start | bytes 772
  152.0 33.1 %copy-start.26 = (f32[64]{0:T(128)S(1)}, f32[64]{0:T(128)}, u32[]{:S(2)}) copy-start(f32[64]{0:T(128)} %param.83) | copy-start | bytes 772
  (1 other events, 0.7 us)
where the time goes:
time: 186 us; the launch traced here: 185 us
  Pallas kernels  80.9 us (43%)
  waiting for transfers between devices  58.8 us (32%)
  starting transfers between devices  39 us (21%)
  other arithmetic  2.79 us (2%)
  between operations  2.25 us (1%)
    ppermute x3, waiting for transfers between devices, to_all(): lax.ppermute(second, 'hidden', [(i, (i + 2 * k) % NH) for i in range(NH)])  24.8 us
    pallas_call x1, Pallas kernels, gather(): pl.pallas_call(gather_kernel, out_shape=(sds((ROWS, 128), F32), sds((ROWS...  23.9 us
    all_to_all x1, waiting for transfers between devices, fast(): lax.all_to_all(lists, 'hidden', split_axis=0, concat_axis=0, tiled=True)  18.6 us
    all_to_all x2, starting transfers between devices, exchange(): a = lax.all_to_all(a, 'patch', split_axis=0, concat_axis=0, tiled=True)  12.2 us
    ppermute x2, waiting for transfers between devices, exchange(): p = lax.ppermute(p, 'patch', first)  11.4 us
    pallas_call x1, Pallas kernels, pack(): pl.pallas_call(pack_kernel, grid=(1,), in_specs=[pl.BlockSpec(memory_spac...  9.56 us
    pallas_call x1, Pallas kernels, nodes(): pl.pallas_call(nodes_kernel, grid_spec=pltpu.PrefetchScalarGridSpec(num_s...  9.36 us
    pallas_call x1, Pallas kernels, finish(): pl.pallas_call(finish_kernel, in_specs=[smem, vmem, vmem, vmem], out_spec...  8.59 us
  transfers between devices with their start and end apart: 12, of which 6 were waited for; matrix products, arithmetic and copies ran while one was open for 2% of the time, Pallas kernels for 30%

commit v1 on v0

--- a/solution.py
+++ b/solution.py
@@ -163,31 +163,35 @@
     total = starts[ROWS, own]
 
     def compact(i, carry):
-        @pl.when(i % 2 == 0)
-        def _():
-            chunk(i // 2).wait()
-
-        parts = [known[k, pl.ds(pl.multiple_of(8 * (i // 2), 8), 8), :] for k in range(7)]
-        odd = i % 2 == 1
-        parts = [jnp.where(odd, x[4:8], x[0:4]) for x in parts]
-        c_row = row_of(parts[6])
-        facts = jnp.concatenate([row_of(x) for x in parts[:6]] + [jnp.zeros((2, 512), F32)], axis=0).astype(BF)
-        source = pl.ds(pl.multiple_of(512 * i, 512), 512)
-        first = starts[4 * i, own]
-        last = jnp.where(i == 15, total, starts[jnp.minimum(4 * i + 4, ROWS - 1), own] + 16)
-        rounds = (jnp.minimum(last, N1) - first + STEP - 1) // STEP
-
-        def add(k, carry):
-            at = pl.multiple_of(first + STEP * k, 16)
-            hit = onehot(c_row == (iota((STEP, 512), 0) + at).astype(F32))
-            acc[pl.ds(at, STEP), :] += dot(hit, edge[source, :])
-            meta[pl.ds(at, STEP), :] += dot_nt(hit, facts)
-            return carry
-
-        lax.fori_loop(0, rounds, add, 0)
+        chunk(i).wait()
+        parts = [known[k, pl.ds(pl.multiple_of(8 * i, 8), 8), :] for k in range(7)]
+        for half in range(2):
+            rows = slice(4 * half, 4 * half + 4)
+            c_row = row_of(parts[6][rows])
+            facts = [row_of(x[rows]) for x in parts[:6]] + [jnp.zeros((2, 512), F32)]
+            facts = jnp.concatenate(facts, axis=0).astype(BF)
+            source = pl.ds(pl.multiple_of(1024 * i + 512 * half, 512), 512)
+
+            def add(at, c_row=c_row, facts=facts, source=source):
+                hit = onehot(c_row == (iota((STEP, 512), 0) + at).astype(F32))
+                acc[pl.ds(at, STEP), :] += dot(hit, edge[source, :])
+                meta[pl.ds(at, STEP), :] += dot_nt(hit, facts)
+
+            first = starts[8 * i + 4 * half, own]
+            last = starts[jnp.minimum(8 * i + 4 * half + 4, ROWS - 1), own] + 16
+            if half == 1:
+                last = jnp.where(i == 7, total, last)
+            rounds = (jnp.minimum(last, N1) - first + STEP - 1) // STEP
+            add(pl.multiple_of(jnp.minimum(first, N1), 16))
+
+            def more(k, carry, first=first, add=add):
+                add(pl.multiple_of(first + STEP * k, 16))
+                return carry
+
+            lax.fori_loop(1, rounds, more, 0)
         return carry
 
-    lax.fori_loop(0, 16, compact, 0)
+    lax.fori_loop(0, 8, compact, 0)
     grid_copy.wait()
     T = 384
     lower = onehot(iota((T, T), 1) < iota((T, T), 0))
@@ -318,13 +322,9 @@
     w_sender = jnp.concatenate([first_ref[n, 64:128, :] for n in order], axis=0)
     bias = vectors_of(first_ref.at[:, VROW:WROWS], 0, order)[0]
     T = 384
-
-    def first_layer(i, carry):
-        at = pl.ds(pl.multiple_of(T * i, T), T)
+    for i in range(N1 // T):
+        at = slice(T * i, T * i + T)
         pre[at, 0:D] = (dot_nt(list_ref[at, :], w_edge) + dot_nt(sent_ref[at, :], w_sender) + bias).astype(BF)
-        return carry
-
-    lax.fori_loop(0, N1 // T, first_layer, 0)
     pre[:, D : D + 128] = info_ref[...]
 
     def spread(i, carry):

time: 186 us -> 185 us (level)
  no operation moved by 1% of the time
where the time goes in v1:
time: 185 us
  Pallas kernels  80 us (43%)
  waiting for transfers between devices  58.8 us (32%)
  starting transfers between devices  39 us (21%)
  other arithmetic  2.79 us (2%)
  between operations  2.29 us (1%)
    ppermute x3, waiting for transfers between devices, to_all(): lax.ppermute(second, 'hidden', [(i, (i + 2 * k) % NH) for i in range(NH)])  24.8 us
    pallas_call x1, Pallas kernels, gather(): pl.pallas_call(gather_kernel, out_shape=(sds((ROWS, 128), F32), sds((ROWS...  23.5 us
    all_to_all x1, waiting for transfers between devices, fast(): lax.all_to_all(lists, 'hidden', split_axis=0, concat_axis=0, tiled=True)  18.6 us
    all_to_all x2, starting transfers between devices, exchange(): a = lax.all_to_all(a, 'patch', split_axis=0, concat_axis=0, tiled=True)  12.2 us
    ppermute x2, waiting for transfers between devices, exchange(): p = lax.ppermute(p, 'patch', first)  11.4 us
    pallas_call x1, Pallas kernels, nodes(): pl.pallas_call(nodes_kernel, grid_spec=pltpu.PrefetchScalarGridSpec(num_s...  9.36 us
    pallas_call x1, Pallas kernels, pack(): pl.pallas_call(pack_kernel, grid=(1,), in_specs=[pl.BlockSpec(memory_spac...  9.01 us
    pallas_call x1, Pallas kernels, finish(): pl.pallas_call(finish_kernel, in_specs=[smem, vmem, vmem, vmem], out_spec...  8.59 us
  transfers between devices with their start and end apart: 12, of which 6 were waited for; matrix products, arithmetic and copies ran while one was open for 2% of the time, Pallas kernels for 30%

profile of v1, /device:TPU:1, one launch (start us, length us, event | category | flops | bytes accessed | tf_op | source)
XLA Modules:
  0.0 184.6 jit_solution(18003820848102463123)
XLA Ops:
  0.7 2.5 %stacked.1 = (bf16[8,136,512]{2,1,0:T(8,128)(2,1)}, bf16[320,512]{1,0:T(8,128)(2,1)}) custom-call(bf16[64,512]{1,0:T(8,128)(2,1)} %bitcast.205, bf16[64,512]{1,0:T(8,128)(2,1)} %bitcast.206, bf16[64,512]{1,0:T(8,128)(2,1)} %bitcast.207, bf16[64,512]{1,0:T(8,128)(2,1)} %bitcast.208, bf16[64,512]{1,0:T(8,128)(2,1)} %bitcast.209, bf16[64,512]{1,0:T(8,128)(2,1)} %eo.1, ...), custom_call_target="tpu_custom_call" | custom-call | tf_op jit(solution)/shard_map/stacked/pallas_call | solution.py:302
  3.1 5.8 %all-to-all-start.5 = ((bf16[8,136,512]{2,1,0:T(8,128)(2,1)}), bf16[8,136,512]{2,1,0:T(8,128)(2,1)}, u32[]{:S(2)}, u32[]{:S(2)}) async-start(bf16[8,136,512]{2,1,0:T(8,128)(2,1)} %get-tuple-element.2240), calls=%async_computation.5 | async-start | bytes 2228224 | tf_op jit(solution)/shard_map/all_to_all | solution.py:310
  8.9 1.4 collective-permute-start.4
  10.3 2.4 %collective-permute-start.5 = (bf16[320,512]{1,0:T(8,128)(2,1)}, bf16[320,512]{1,0:T(8,128)(2,1)S(1)}, u32[]{:S(2)}, u32[]{:S(2)}) collective-permute-start(bf16[320,512]{1,0:T(8,128)(2,1)} %get-tuple-element.2245), channel_id=1, source_target_pairs={{0,4},{1,5},{2,6},{3,7},{4,0},{5,1},{6,2},{7,3},{8,12},{9,13},{10,... | collective-permute-start | bytes 983048 | tf_op jit(solution)/shard_map/ppermute | solution.py:313
  13.9 17.7 %collective-permute-done.4 = bf16[320,512]{1,0:T(8,128)(2,1)S(1)} collective-permute-done((bf16[320,512]{1,0:T(8,128)(2,1)}, bf16[320,512]{1,0:T(8,128)(2,1)S(1)}, u32[]{:S(2)}, u32[]{:S(2)}) %collective-permute-start.4) | collective-permute-done | bytes 327712 | tf_op jit(solution)/shard_map/ppermute | solution.py:313
  31.5 7.2 %collective-permute-done.5 = bf16[320,512]{1,0:T(8,128)(2,1)S(1)} collective-permute-done((bf16[320,512]{1,0:T(8,128)(2,1)}, bf16[320,512]{1,0:T(8,128)(2,1)S(1)}, u32[]{:S(2)}, u32[]{:S(2)}) %collective-permute-start.5) | collective-permute-done | bytes 327712 | tf_op jit(solution)/shard_map/ppermute | solution.py:313
  38.7 2.2 %pad_maximum_fusion.wr_ref.wo_ref.wi_ref.wm_ref = bf16[4,320,512]{2,1,0:T(8,128)(2,1)} fusion(bf16[1,320,512]{2,1,0:T(8,128)(2,1)S(1)} %bitcast.204, bf16[1,320,512]{2,1,0:T(8,128)(2,1)S(1)} %bitcast.203, bf16[1,320,512]{2,1,0:T(8,128)(2,1)S(1)} %bitcast.202, bf16[1,320,512]{2,1,0:T(8,128)(2,1)} %bitcast.201), kind=kLoop, calls=%fused_computation.151 | loop fusion | flops 1966080 | bytes 2621440 | tf_op jit(solution)/shard_map/stack | solution.py:314
  43.1 23.5 %gather.1 = (f32[64,128]{1,0:T(8,128)}, s32[72,128]{1,0:T(8,128)}, bf16[1152,512]{1,0:T(8,128)(2,1)}, bf16[1152,512]{1,0:T(8,128)(2,1)}, bf16[1152,128]{1,0:T(8,...) custom-call(s32[1]{0:T(128)S(6)} %copy.458.count_ref, s32[2]{0:T(128)} %pad_add_fusion.where_ref, ...), custom_call_target="tpu_custom_call" | custom-call | tf_op jit(solution)/shard_map/gather/pallas_call | solution.py:237
  66.6 9.0 %pack.1 = (bf16[16,72,512]{2,1,0:T(8,128)(2,1)}, bf16[168,512]{1,0:T(8,128)(2,1)}, bf16[168,512]{1,0:T(8,128)(2,1)}, bf16[1152,640]{1,0:T(8,128)(2,1)}) custom-call(s32[2]{0:T(128)} %pad_add_fusion.where_ref, bf16[1152,512]{1,0:T(8,128)(2,1)} %get-tuple-element.2236.list_ref, bf16[1152,512]{1,0:T(8,128)(2,1)} %get-tuple-element.2237.sent_ref, ...), custom_call_target="tpu_custom_call" | custom-call | tf_op jit(solution)/shard_map/pack/pallas_call | solution.py:363
  75.6 7.8 %all-to-all-start.6 = ((bf16[16,72,512]{2,1,0:T(8,128)(2,1)}), bf16[16,72,512]{2,1,0:T(8,128)(2,1)}, u32[]{:S(2)}, u32[]{:S(2)}) async-start(bf16[16,72,512]{2,1,0:T(8,128)(2,1)} %get-tuple-element.2241), calls=%async_computation.6 | async-start | bytes 2359296 | tf_op jit(solution)/shard_map/all_to_all | solution.py:677
  84.8 3.5 %collective-permute-start.3 = (bf16[168,512]{1,0:T(8,128)(2,1)}, bf16[168,512]{1,0:T(8,128)(2,1)S(1)}, u32[]{:S(2)}, u32[]{:S(2)}) collective-permute-start(bf16[168,512]{1,0:T(8,128)(2,1)} %get-tuple-element.2243), channel_id=1, source_target_pairs={{0,120},{8,0},{16,8},{24,16},{32,24},{40,32},{48,40},{56,48},{64,5... | collective-permute-start | bytes 516104 | tf_op jit(solution)/shard_map/ppermute | solution.py:676
  88.3 7.5 %local.1 = (bf16[640,512]{1,0:T(8,128)(2,1)}, bf16[384,512]{1,0:T(8,128)(2,1)}, f32[8,384]{1,0:T(8,128)}) custom-call(s32[2]{0:T(128)} %pad_add_fusion.where_ref, bf16[1152,640]{1,0:T(8,128)(2,1)} %get-tuple-element.2244.pre_ref, f32[8,1280]{1,0:T(8,128)} %get-tuple-element.2239.slot_row_ref, bf16[5120,512]{1,0:T(8,128)(2,1)} %mesh_ref.3, ...), custom_call_target="tpu_custom_call" | custom-call | tf_op jit(solution)/shard_map/local/pallas_call | solution.py:420
  95.8 9.6 %collective-permute-done.2.rp_ref = bf16[168,512]{1,0:T(8,128)(2,1)S(1)} collective-permute-done((bf16[168,512]{1,0:T(8,128)(2,1)}, bf16[168,512]{1,0:T(8,128)(2,1)S(1)}, u32[]{:S(2)}, u32[]{:S(2)}) %collective-permute-start.2) | collective-permute-done | bytes 172064 | tf_op jit(solution)/shard_map/ppermute | solution.py:675
  106.2 7.7 %owner.1 = (bf16[16,64,512]{2,1,0:T(8,128)(2,1)}, bf16[160,512]{1,0:T(8,128)(2,1)}, bf16[160,512]{1,0:T(8,128)(2,1)}, f32[8,1536]{1,0:T(8,128)}, f32[8,128]{1,0:T(8,128)}) custom-call(bf16[16,72,512]{2,1,0:T(8,128)(2,1)} %all-to-all-done.6.ra_ref, bf16[168,512]{1,0:T(8,128)(2,1)} %copy-done.12, bf16[168,512]{1,0:T(8,128)(2,1)} %copy-done.13, ...), custom_call_target="tpu_custom_call" | custom-call | tf_op jit(solution)/shard_map/owner/pallas_call | solution.py:484
  113.8 4.3 %all-to-all-start.7 = ((bf16[16,64,512]{2,1,0:T(8,128)(2,1)}), bf16[16,64,512]{2,1,0:T(8,128)(2,1)}, u32[]{:S(2)}, u32[]{:S(2)}) async-start(bf16[16,64,512]{2,1,0:T(8,128)(2,1)} %get-tuple-element.2247.oa_ref), calls=%async_computation.7 | async-start | bytes 2097152 | tf_op jit(solution)/shard_map/all_to_all | solution.py:677
  118.2 4.6 %collective-permute-start.8 = (bf16[160,512]{1,0:T(8,128)(2,1)}, bf16[160,512]{1,0:T(8,128)(2,1)S(1)}, u32[]{:S(2)}, u32[]{:S(2)}) collective-permute-start(bf16[160,512]{1,0:T(8,128)(2,1)} %get-tuple-element.2248.op_ref), channel_id=1, source_target_pairs={{0,120},{8,0},{16,8},{24,16},{32,24},{40,32},{48,40},{56,48},{64,5... | collective-permute-start | bytes 491528 | tf_op jit(solution)/shard_map/ppermute | solution.py:675
  122.8 9.4 %nodes.1.mesh_ref = bf16[8,320,128]{2,1,0:T(8,128)(2,1)} custom-call(s32[2]{0:T(128)} %pad_add_fusion.where_ref, bf16[16,64,512]{2,1,0:T(8,128)(2,1)} %get-tuple-element.2247.oa_ref, bf16[160,512]{1,0:T(8,128)(2,1)} %get-tuple-element.2248.op_ref, bf16[160,512]{1,0:T(8,128)(2,1)} %get-tuple-element.2249.om_ref, ...), custom_call_target="tpu_custom_call" | custom-call | tf_op jit(solution)/shard_map/nodes/pallas_call | solution.py:534
  132.2 1.8 collective-permute-done.8.mp_ref
  134.0 3.9 %collective-permute-done.9.mm_ref = bf16[160,512]{1,0:T(8,128)(2,1)S(1)} collective-permute-done((bf16[160,512]{1,0:T(8,128)(2,1)}, bf16[160,512]{1,0:T(8,128)(2,1)S(1)}, u32[]{:S(2)}, u32[]{:S(2)}) %collective-permute-start.9) | collective-permute-done | bytes 163872 | tf_op jit(solution)/shard_map/ppermute | solution.py:676
  138.6 6.7 %unpack.1 = bf16[8,912,128]{2,1,0:T(8,128)(2,1)} custom-call(bf16[16,64,512]{2,1,0:T(8,128)(2,1)} %all-to-all-done.7.ma_ref, bf16[160,512]{1,0:T(8,128)(2,1)} %copy-done.14, bf16[160,512]{1,0:T(8,128)(2,1)} %copy-done.15, bf16[384,512]{1,0:T(8,128)(2,1)} %get-tuple-element.2250.own_msg_ref.ms_ref, f32[1152,8]{1,0:T(8,128)} %get-tuple-element.2251.slot_ref, ...), custom_call_target="tpu_custom_call" | custom-call | tf_op jit(solution)/shard_map/unpack/pallas_call | solution.py:580
  145.2 5.7 %all-to-all-start.8 = ((bf16[8,912,128]{2,1,0:T(8,128)(2,1)}), bf16[8,912,128]{2,1,0:T(8,128)(2,1)}, u32[]{:S(2)}, u32[]{:S(2)}) async-start(bf16[8,912,128]{2,1,0:T(8,128)(2,1)} %unpack.1), calls=%async_computation.8 | async-start | bytes 3735552 | tf_op jit(solution)/shard_map/all_to_all | solution.py:706
  151.0 5.2 %columns.1.column_ref = bf16[64,8192]{1,0:T(8,128)(2,1)} custom-call(s32[2]{0:T(128)} %pad_add_fusion.where_ref, bf16[8192,512]{1,0:T(8,128)(2,1)} %edge_ref.1), custom_call_target="tpu_custom_call" | custom-call | tf_op jit(solution)/shard_map/columns/pallas_call | solution.py:602
  156.2 18.6 %all-to-all-done.8.in_ref = bf16[8,912,128]{2,1,0:T(8,128)(2,1)} async-done(((bf16[8,912,128]{2,1,0:T(8,128)(2,1)}), bf16[8,912,128]{2,1,0:T(8,128)(2,1)}, u32[]{:S(2)}, u32[]{:S(2)}) %all-to-all-start.8) | async-done | bytes 1867808 | tf_op jit(solution)/shard_map/all_to_all | solution.py:706
  174.9 8.6 %finish.1 = (bf16[64,8192]{1,0:T(8,128)(2,1)}, bf16[64,5120]{1,0:T(8,128)(2,1)}, s32[1,1]{1,0:T(1,128)}) custom-call(s32[72,128]{1,0:T(8,128)} %get-tuple-element.2235.starts_ref, bf16[8,912,128]{2,1,0:T(8,128)(2,1)} %all-to-all-done.8.in_ref, f32[64,128]{1,0:T(8,128)} %get-tuple-element.2255.key_ref, bf16[64,8192]{1,0:T(8,128)(2,1)} %columns.1.column_ref), custom_call_target="tpu_custom_call" | custom-call | tf_op jit(solution)/shard_map/finish/pallas_call | solution.py:660
  (38 shorter events, 5.8 us)
Async XLA Ops:
  0.6 42.5 %copy-start.16 = (s32[8192]{0:T(1024)S(1)}, s32[8192]{0:T(1024)}, u32[]{:S(2)}) copy-start(s32[8192]{0:T(1024)} %param.69) | copy-start | bytes 98308
  0.6 42.5 %copy-start = (bf16[3072,512]{1,0:T(8,128)(2,1)S(1)}, bf16[3072,512]{1,0:T(8,128)(2,1)}, u32[]{:S(2)}) copy-start(bf16[3072,512]{1,0:T(8,128)(2,1)} %grid_hbm.1) | copy-start | bytes 9437188
  3.1 63.4 %all-to-all-start.5 = ((bf16[8,136,512]{2,1,0:T(8,128)(2,1)}), bf16[8,136,512]{2,1,0:T(8,128)(2,1)}, u32[]{:S(2)}, u32[]{:S(2)}) async-start(bf16[8,136,512]{2,1,0:T(8,128)(2,1)} %get-tuple-element.2240), calls=%async_computation.5 | async-start | bytes 2228224 | tf_op jit(solution)/shard_map/all_to_all | solution.py:310
  8.9 22.6 %collective-permute-start.4 = (bf16[320,512]{1,0:T(8,128)(2,1)}, bf16[320,512]{1,0:T(8,128)(2,1)S(1)}, u32[]{:S(2)}, u32[]{:S(2)}) collective-permute-start(bf16[320,512]{1,0:T(8,128)(2,1)} %get-tuple-element.2245), channel_id=1, source_target_pairs={{0,2},{1,3},{2,4},{3,5},{4,6},{5,7},{6,0},{7,1},{8,10},{9,11},{10,... | collective-permute-start | bytes 983048 | tf_op jit(solution)/shard_map/ppermute | solution.py:313
  10.3 28.4 %collective-permute-start.5 = (bf16[320,512]{1,0:T(8,128)(2,1)}, bf16[320,512]{1,0:T(8,128)(2,1)S(1)}, u32[]{:S(2)}, u32[]{:S(2)}) collective-permute-start(bf16[320,512]{1,0:T(8,128)(2,1)} %get-tuple-element.2245), channel_id=1, source_target_pairs={{0,4},{1,5},{2,6},{3,7},{4,0},{5,1},{6,2},{7,3},{8,12},{9,13},{10,... | collective-permute-start | bytes 983048 | tf_op jit(solution)/shard_map/ppermute | solution.py:313
  12.7 26.0 %collective-permute-start.6 = (bf16[320,512]{1,0:T(8,128)(2,1)}, bf16[320,512]{1,0:T(8,128)(2,1)S(1)}, u32[]{:S(2)}, u32[]{:S(2)}) collective-permute-start(bf16[320,512]{1,0:T(8,128)(2,1)} %get-tuple-element.2245), channel_id=1, source_target_pairs={{0,6},{1,7},{2,0},{3,1},{4,2},{5,3},{6,4},{7,5},{8,14},{9,15},{10,... | collective-permute-start | bytes 983048 | tf_op jit(solution)/shard_map/ppermute | solution.py:313
  40.9 47.4 %collective-permute-start.7 = (bf16[4,320,512]{2,1,0:T(8,128)(2,1)}, bf16[4,320,512]{2,1,0:T(8,128)(2,1)}, u32[]{:S(2)}, u32[]{:S(2)}) collective-permute-start(bf16[4,320,512]{2,1,0:T(8,128)(2,1)} %pad_maximum_fusion.wr_ref.wo_ref.wi_ref.wm_ref), channel_id=1, source_target_pairs={{0,1},{1,0},{2,3},{3,2},{4,5},{5,4},{6,7},{7,6},{8,9},{9,8},{10,11... | collective-permute-start | bytes 3932168 | tf_op jit(solution)/shard_map/ppermute | solution.py:315
  75.6 29.8 %all-to-all-start.6 = ((bf16[16,72,512]{2,1,0:T(8,128)(2,1)}), bf16[16,72,512]{2,1,0:T(8,128)(2,1)}, u32[]{:S(2)}, u32[]{:S(2)}) async-start(bf16[16,72,512]{2,1,0:T(8,128)(2,1)} %get-tuple-element.2241), calls=%async_computation.6 | async-start | bytes 2359296 | tf_op jit(solution)/shard_map/all_to_all | solution.py:677
  83.4 22.0 %collective-permute-start.2 = (bf16[168,512]{1,0:T(8,128)(2,1)}, bf16[168,512]{1,0:T(8,128)(2,1)S(1)}, u32[]{:S(2)}, u32[]{:S(2)}) collective-permute-start(bf16[168,512]{1,0:T(8,128)(2,1)} %get-tuple-element.2242), channel_id=1, source_target_pairs={{0,8},{8,16},{16,24},{24,32},{32,40},{40,48},{48,56},{56,64},{64,7... | collective-permute-start | bytes 516104 | tf_op jit(solution)/shard_map/ppermute | solution.py:675
  84.8 20.7 %collective-permute-start.3 = (bf16[168,512]{1,0:T(8,128)(2,1)}, bf16[168,512]{1,0:T(8,128)(2,1)S(1)}, u32[]{:S(2)}, u32[]{:S(2)}) collective-permute-start(bf16[168,512]{1,0:T(8,128)(2,1)} %get-tuple-element.2243), channel_id=1, source_target_pairs={{0,120},{8,0},{16,8},{24,16},{32,24},{40,32},{48,40},{56,48},{64,5... | collective-permute-start | bytes 516104 | tf_op jit(solution)/shard_map/ppermute | solution.py:676
  105.4 0.8 copy-start.13
  113.8 24.1 %all-to-all-start.7 = ((bf16[16,64,512]{2,1,0:T(8,128)(2,1)}), bf16[16,64,512]{2,1,0:T(8,128)(2,1)}, u32[]{:S(2)}, u32[]{:S(2)}) async-start(bf16[16,64,512]{2,1,0:T(8,128)(2,1)} %get-tuple-element.2247.oa_ref), calls=%async_computation.7 | async-start | bytes 2097152 | tf_op jit(solution)/shard_map/all_to_all | solution.py:677
  118.2 15.8 %collective-permute-start.8 = (bf16[160,512]{1,0:T(8,128)(2,1)}, bf16[160,512]{1,0:T(8,128)(2,1)S(1)}, u32[]{:S(2)}, u32[]{:S(2)}) collective-permute-start(bf16[160,512]{1,0:T(8,128)(2,1)} %get-tuple-element.2248.op_ref), channel_id=1, source_target_pairs={{0,120},{8,0},{16,8},{24,16},{32,24},{40,32},{48,40},{56,48},{64,5... | collective-permute-start | bytes 491528 | tf_op jit(solution)/shard_map/ppermute | solution.py:675
  122.8 15.1 %collective-permute-start.9 = (bf16[160,512]{1,0:T(8,128)(2,1)}, bf16[160,512]{1,0:T(8,128)(2,1)S(1)}, u32[]{:S(2)}, u32[]{:S(2)}) collective-permute-start(bf16[160,512]{1,0:T(8,128)(2,1)} %get-tuple-element.2249.om_ref), channel_id=1, source_target_pairs={{0,8},{8,16},{16,24},{24,32},{32,40},{40,48},{48,56},{56,64},{64,7... | collective-permute-start | bytes 491528 | tf_op jit(solution)/shard_map/ppermute | solution.py:676
  134.0 3.9 %copy-start.14 = (bf16[160,512]{1,0:T(8,128)(2,1)}, bf16[160,512]{1,0:T(8,128)(2,1)S(1)}, u32[]{:S(2)}) copy-start(bf16[160,512]{1,0:T(8,128)(2,1)S(1)} %collective-permute-done.8.mp_ref) | copy-start | bytes 491524
  137.9 0.7 copy-start.15
  145.2 29.6 %all-to-all-start.8 = ((bf16[8,912,128]{2,1,0:T(8,128)(2,1)}), bf16[8,912,128]{2,1,0:T(8,128)(2,1)}, u32[]{:S(2)}, u32[]{:S(2)}) async-start(bf16[8,912,128]{2,1,0:T(8,128)(2,1)} %unpack.1), calls=%async_computation.8 | async-start | bytes 3735552 | tf_op jit(solution)/shard_map/all_to_all | solution.py:706
  151.0 33.1 %copy-start.8 = (bf16[512,64]{0,1:T(8,128)(2,1)S(1)}, bf16[512,64]{0,1:T(8,128)(2,1)}, u32[]{:S(2)}) copy-start(bf16[512,64]{0,1:T(8,128)(2,1)} %param.73) | copy-start | bytes 196612
  151.0 33.1 %copy-start.17 = (s32[8192]{0:T(1024)S(1)}, s32[8192]{0:T(1024)}, u32[]{:S(2)}) copy-start(s32[8192]{0:T(1024)} %param.69) | copy-start | bytes 98308
  151.0 33.1 %copy-start.20 = (f32[64,128]{1,0:T(8,128)S(1)}, f32[64,128]{1,0:T(8,128)}, u32[]{:S(2)}) copy-start(f32[64,128]{1,0:T(8,128)} %get-tuple-element.2259) | copy-start | bytes 98308
  151.0 33.1 %copy-start.21 = (f32[64]{0:T(128)S(1)}, f32[64]{0:T(128)}, u32[]{:S(2)}) copy-start(f32[64]{0:T(128)} %param.79) | copy-start | bytes 772
  151.0 33.1 %copy-start.22 = (f32[64]{0:T(128)S(1)}, f32[64]{0:T(128)}, u32[]{:S(2)}) copy-start(f32[64]{0:T(128)} %param.80) | copy-start | bytes 772
  151.0 33.1 %copy-start.25 = (f32[64]{0:T(128)S(1)}, f32[64]{0:T(128)}, u32[]{:S(2)}) copy-start(f32[64]{0:T(128)} %param.76) | copy-start | bytes 772
  151.0 33.1 %copy-start.26 = (f32[64]{0:T(128)S(1)}, f32[64]{0:T(128)}, u32[]{:S(2)}) copy-start(f32[64]{0:T(128)} %param.83) | copy-start | bytes 772
  (1 other events, 0.7 us)
